TPU v7x, 32 devices: a whole 2x2x4 slice. The times are simulated.
32 devices in a mesh: sp: 4 (over x, core), tp: 8 (over z, y).
Axes of the slice: x: 2, y: 2, z: 4, core: 2. Of those that a mesh axis runs over, the one named last changes fastest.
Arguments:
- tokens: bfloat16 [8, 220, 4096], P(None, 'sp'), may hold values from -6 to 6
- modulation: float32 [6, 4096], replicated, may hold values from -2.5 to 2.5
- w_qkv: bfloat16 [4096, 3, 4096], P('sp', None, 'tp'), may hold values from -4 to 4
- w_out: bfloat16 [4096, 4096], P('tp', 'sp'), may hold values from -0.09375 to 0.09375
- w_up: bfloat16 [4096, 16384], P('sp', 'tp'), may hold values from -0.09375 to 0.09375
- w_down: bfloat16 [16384, 4096], P('tp', 'sp'), may hold values from -0.046875 to 0.046875
Outputs:
- block_out: bfloat16 [8, 220, 4096], P(None, 'sp', 'tp')
All inputs are finite; a program needn't handle non-finite values.
Results may differ from a plain program's by a relative error of at most 0.012.
Values may be sent and summed in bfloat16 or wider, within the bound.
No kernel may reach another device: no remote copies, remote signals or barrier semaphores. Data moves between devices by JAX's collectives and lax.ppermute only.
A program may use at most 128 MiB of HBM per device.

v0:
```python
import jax
import jax.numpy as jnp
from jax import lax
from jax.sharding import PartitionSpec as P

DH = 128
EPSILON = 1e-06


def normalize(tok_rows, shift_vec, scale_vec):
    values = tok_rows.astype(jnp.float32)
    center = jnp.mean(values, axis=-1, keepdims=True)
    spread = jnp.mean(jnp.square(values - center), axis=-1, keepdims=True)
    scaled = (values - center) * lax.rsqrt(spread + EPSILON)
    return (scaled * (1.0 + scale_vec) + shift_vec).astype(jnp.bfloat16)


def project_rows(operand, weight, einsum_form):
    return jnp.einsum(
        einsum_form,
        operand,
        lax.all_gather(weight, "sp", axis=0, tiled=True),
        preferred_element_type=jnp.float32,
    )


def project_cols(operand, weight, einsum_form, leading):
    portion = lax.all_gather(weight, "sp", axis=1, tiled=True)
    shaped = portion.reshape(leading + (portion.shape[1],))
    return jnp.einsum(einsum_form, operand, shaped, preferred_element_type=jnp.float32)


def attend_items(pieces):
    queries, key_rows, values = pieces
    factor = queries.shape[-1] ** (-0.5)

    def single(triple):
        query_one, key_one, value_one = triple
        scores = (
            lax.dot_general(
                query_one, key_one, (((1,), (1,)), ((), ())), preferred_element_type=jnp.float32
            )
            * factor
        )
        row_max = jnp.max(scores, axis=1, keepdims=True)
        raw_weights = jnp.exp(scores - row_max)
        att_weights = (raw_weights / jnp.sum(raw_weights, axis=1, keepdims=True)).astype(
            jnp.bfloat16
        )
        return jnp.dot(att_weights, value_one, preferred_element_type=jnp.float32).astype(
            jnp.bfloat16
        )

    result = lax.map(single, (queries[0], key_rows[0], values[0]))
    return result[None]


def attention_combine(base, partial_value, gate):
    summed = lax.psum(partial_value.astype(jnp.bfloat16), "tp").astype(jnp.float32)
    full = (base.astype(jnp.float32) + gate * summed).astype(jnp.bfloat16)
    return full


def mlp_combine(base, partial_value, gate):
    tp_count = lax.axis_size("tp")
    width = base.shape[2] // tp_count
    offset = lax.axis_index("tp") * width
    base_mine = lax.dynamic_slice_in_dim(base, offset, width, 2).astype(jnp.float32)
    gate_mine = lax.dynamic_slice_in_dim(gate, offset, width, 0)
    share = lax.psum_scatter(
        partial_value.astype(jnp.bfloat16), "tp", scatter_dimension=2, tiled=True
    ).astype(jnp.float32)
    return (base_mine + gate_mine * share).astype(jnp.bfloat16)


def shards(tokens, modulation, w_qkv, w_out, w_up, w_down):
    frames, patches, width = tokens.shape
    heads_local = w_qkv.shape[2] // DH
    sp_count = lax.axis_size("sp")
    items_dev = heads_local * frames // sp_count
    mod_a = normalize(tokens, modulation[0], modulation[1])
    weight_qkv = w_qkv.reshape(w_qkv.shape[0], 3, heads_local, DH)
    projected = project_rows(mod_a, weight_qkv, "fpd,dshe->shfpe").astype(jnp.bfloat16)
    projected = projected.reshape(3, sp_count, items_dev, patches, DH)
    attended = attend_items(
        (
            lax.all_to_all(projected[0], "sp", split_axis=0, concat_axis=2, tiled=True),
            lax.all_to_all(projected[1], "sp", split_axis=0, concat_axis=2, tiled=True),
            lax.all_to_all(projected[2], "sp", split_axis=0, concat_axis=2, tiled=True),
        )
    )
    returned = lax.all_to_all(attended, "sp", split_axis=2, concat_axis=0, tiled=True)
    returned = returned.reshape(heads_local, frames, patches, DH)
    partial_attn = project_cols(returned, w_out, "hfpd,hde->fpe", (heads_local, DH))
    middle = attention_combine(tokens, partial_attn, modulation[2])
    mod_b = normalize(middle, modulation[3], modulation[4])
    up_proj = project_rows(mod_b, w_up, "fpd,dc->fpc")
    hidden = jax.nn.gelu(up_proj, approximate=True).astype(jnp.bfloat16)
    partial_mlp = project_cols(hidden, w_down, "fpk,kc->fpc", (w_down.shape[0],))
    return mlp_combine(middle, partial_mlp, modulation[5])


def solution(mesh):
    placed = (
        P(None, "sp", None),
        P(),
        P("sp", None, "tp"),
        P("tp", "sp"),
        P("sp", "tp"),
        P("tp", "sp"),
    )
    return jax.shard_map(
        shards, mesh=mesh, in_specs=placed, out_specs=P(None, "sp", "tp"), check_vma=False
    )
```

profile of v0, /device:TPU:0, one launch (start us, length us, event | category | flops | bytes accessed | tf_op | source)
XLA Modules:
  0.0 655.9 jit_solution(7131236097919553995)
XLA Ops:
  6.5 3.2 copy.22
  9.7 2.8 copy.23
  12.6 0.7 all-gather.7.cloned.1.call-update
  13.4 5.8 convert_reduce_fusion
  19.2 3.9 fusion.23
  23.1 74.4 %all-gather.5.cloned.1.call-done = bf16[4096,3,4,128]{3,0,2,1:T(8,128)(2,1)} async-done(((bf16[1024,3,4,128]{3,0,2,1:T(8,128)(2,1)}), bf16[4096,3,4,128]{3,0,2,1:T(8,128)(2,1)}) %all-gather.5.cloned.1.call-update) | async-done | bytes 12582928 | tf_op jit(solution)/shard_map/all_gather | solution.py:22
  97.5 18.3 %fusion.69 = bf16[3,4,8,55,128]{4,3,1,0,2:T(8,128)(2,1)S(1)} fusion(bf16[4096,3,4,128]{3,0,2,1:T(8,128)(2,1)} %all-gather.5.cloned.1.call-done, f32[4096]{0:T(1024)S(1)} %bitcast.107, f32[4096]{0:T(1024)S(1)} %bitcast.108, f32[8,55]{1,0:T(8,128)S(1)} %add_rsqrt_fusion.1, f32[8,55]{1,0:T(8,128)S(1)} %broadcast_multiply_fusion.1, bf16[8,55,4096]{2,0,1:T(8,128)(2,1)} %param.8), kind=kOutput, calls=%fused_computation.64 | convolution fusion | flops 5547970560 | bytes 17575360 | tf_op jit(solution)/shard_map/fpd,dshe->shfpe/dot_general | solution.py:19
  115.9 0.9 copy.24
  116.9 3.5 all-to-all-start
  120.3 0.9 copy.25
  121.3 12.3 %all-to-all-done = bf16[4,8,55,128]{3,1,2,0:T(8,128)(2,1)S(1)} async-done(((bf16[4,8,55,128]{3,1,2,0:T(8,128)(2,1)}), bf16[4,8,55,128]{3,1,2,0:T(8,128)(2,1)S(1)}, u32[]{:S(2)}, u32[]{:S(2)}) %all-to-all-start) | async-done | bytes 450592 | tf_op jit(solution)/shard_map/all_to_all | solution.py:87
  133.6 3.5 all-to-all-start.1
  137.1 0.9 copy.26
  138.0 7.0 %all-to-all-done.1 = bf16[4,8,55,128]{3,1,2,0:T(8,128)(2,1)S(1)} async-done(((bf16[4,8,55,128]{3,1,2,0:T(8,128)(2,1)}), bf16[4,8,55,128]{3,1,2,0:T(8,128)(2,1)S(1)}, u32[]{:S(2)}, u32[]{:S(2)}) %all-to-all-start.1) | async-done | bytes 450592 | tf_op jit(solution)/shard_map/all_to_all | solution.py:88
  145.0 3.5 all-to-all-start.2
  148.7 7.8 %all-to-all-done.2 = bf16[4,8,55,128]{3,1,2,0:T(8,128)(2,1)S(1)} async-done(((bf16[4,8,55,128]{3,1,2,0:T(8,128)(2,1)}), bf16[4,8,55,128]{3,1,2,0:T(8,128)(2,1)S(1)}, u32[]{:S(2)}, u32[]{:S(2)}) %all-to-all-start.2) | async-done | bytes 450592 | tf_op jit(solution)/shard_map/all_to_all | solution.py:89
  156.6 4.6 while.10
  156.6 0.2 fusion.89
  156.9 0.2 fusion.91
  157.2 0.2 fusion.89
  157.5 0.2 fusion.91
  157.7 0.2 fusion.89
  158.0 0.2 fusion.91
  158.3 0.2 fusion.89
  158.6 0.2 fusion.91
  158.9 0.2 fusion.89
  159.2 0.2 fusion.91
  159.8 0.2 fusion.91
  160.3 0.2 fusion.91
  160.6 0.2 fusion.89
  160.9 0.2 fusion.91
  161.2 0.9 copy.52
  162.1 3.5 all-to-all-start.3
  165.6 7.9 %all-to-all-done.3 = bf16[1,8,220,128]{3,1,0,2:T(8,128)(2,1)S(1)} async-done(((bf16[1,8,220,128]{3,1,0,2:T(8,128)(2,1)}), bf16[1,8,220,128]{3,1,0,2:T(8,128)(2,1)S(1)}, u32[]{:S(2)}, u32[]{:S(2)}) %all-to-all-start.3) | async-done | bytes 450592 | tf_op jit(solution)/shard_map/all_to_all | solution.py:92
  173.6 5.7 bitcast_convert_fusion
  179.4 0.5 all-gather.11.cloned.1.call-update
  180.0 0.5 all-gather.9.cloned.1.call-update
  180.5 0.3 reduce-scatter.2.cloned.1.call-start
  180.8 141.6 %all-reduce.2.cloned.1.call-done = bf16[8,55,4096]{2,1,0:T(8,128)(2,1)} async-done(((bf16[8,55,4096]{2,1,0:T(8,128)(2,1)}), bf16[8,55,4096]{2,1,0:T(8,128)(2,1)}) %all-reduce.2.cloned.1.call-update) | async-done | bytes 3604496 | tf_op jit(solution)/shard_map/psum | solution.py:59
  322.4 8.3 %convert_reduce_fusion.1 = (f32[8,55]{1,0:T(8,128)S(1)}, bf16[8,55,4096]{2,1,0:T(8,128)(2,1)S(1)}) fusion(bf16[8,55,4096]{2,1,0:T(8,128)(2,1)} %all-reduce.2.cloned.1.call-done, f32[4096]{0:T(1024)S(1)} %bitcast.104, bf16[8,55,4096]{2,0,1:T(8,128)(2,1)} %param.8), kind=kLoop, calls=%fused_computation.27 | loop fusion | flops 12615240 | bytes 10831584 | tf_op jit(solution)/shard_map/reduce_sum | solution.py:12
  330.7 2.0 copy-done.1
  332.7 1.1 fusion.27
  333.8 94.7 %all-gather.11.cloned.1.call-done = bf16[2048,4096]{1,0:T(8,128)(2,1)} async-done(((bf16[2048,1024]{1,0:T(8,128)(2,1)}), bf16[2048,4096]{1,0:T(8,128)(2,1)}) %all-gather.11.cloned.1.call-update) | async-done | bytes 16777232 | tf_op jit(solution)/shard_map/all_gather | solution.py:28
  428.5 107.3 %all-gather.9.cloned.1.call-done = bf16[4096,2048]{1,0:T(8,128)(2,1)} async-done(((bf16[1024,2048]{1,0:T(8,128)(2,1)}), bf16[4096,2048]{1,0:T(8,128)(2,1)}) %all-gather.9.cloned.1.call-update) | async-done | bytes 16777232 | tf_op jit(solution)/shard_map/all_gather | solution.py:22
  535.9 29.4 %fusion.32 = bf16[8,55,4096]{2,1,0:T(8,128)(2,1)} fusion(bf16[2048,4096]{1,0:T(8,128)(2,1)} %all-gather.11.cloned.1.call-done, bf16[4096,2048]{1,0:T(8,128)(2,1)} %all-gather.9.cloned.1.call-done, bf16[8,55,4096]{2,1,0:T(8,128)(2,1)} %copy-done.1, f32[4096]{0:T(1024)S(1)} %bitcast.105, f32[4096]{0:T(1024)S(1)} %bitcast.106, f32[8,55]{1,0:T(8,128)S(1)} %add_rsqrt_fusion, ...), kind=kOutput, calls=%fused_computation.42 | convolution fusion | flops 14784675840 | bytes 40799680 | tf_op jit(solution)/shard_map/fpk,kc->fpc/dot_general | solution.py:30
  565.4 81.5 %reduce-scatter.2.cloned.1.call-done = bf16[8,55,512]{2,1,0:T(8,128)(2,1)} async-done(((bf16[8,55,4096]{2,1,0:T(8,128)(2,1)}), bf16[8,55,512]{2,1,0:T(8,128)(2,1)}) %reduce-scatter.2.cloned.1.call-update) | async-done | bytes 450576 | tf_op jit(solution)/shard_map/reduce_scatter | solution.py:70
  646.9 1.3 add_convert_fusion
  648.2 0.9 copy.32
  (35 shorter events, 1.7 us)
Async XLA Ops:
  6.5 91.0 %all-gather.5.cloned.1.call-start = ((), (), s32[]{:S(2)}) async-start(), calls=%async_computation.5 | async-start | bytes 15728640 | tf_op jit(solution)/shard_map/all_gather | solution.py:22
  9.7 3.6 copy-start.2
  12.6 153.1 %all-gather.7.cloned.1.call-start = ((), (), s32[]{:S(2)}) async-start(), calls=%async_computation.6 | async-start | bytes 5242880 | tf_op jit(solution)/shard_map/all_gather | solution.py:28
  13.3 5.9 copy-start
  116.9 16.7 %all-to-all-start = ((bf16[4,8,55,128]{3,1,2,0:T(8,128)(2,1)}), bf16[4,8,55,128]{3,1,2,0:T(8,128)(2,1)S(1)}, u32[]{:S(2)}, u32[]{:S(2)}) async-start(bf16[4,8,55,128]{3,1,2,0:T(8,128)(2,1)} %copy.24), calls=%async_computation | async-start | bytes 901120 | tf_op jit(solution)/shard_map/all_to_all | solution.py:87
  133.6 11.5 %all-to-all-start.1 = ((bf16[4,8,55,128]{3,1,2,0:T(8,128)(2,1)}), bf16[4,8,55,128]{3,1,2,0:T(8,128)(2,1)S(1)}, u32[]{:S(2)}, u32[]{:S(2)}) async-start(bf16[4,8,55,128]{3,1,2,0:T(8,128)(2,1)} %copy.25), calls=%async_computation.1 | async-start | bytes 901120 | tf_op jit(solution)/shard_map/all_to_all | solution.py:88
  145.0 11.5 %all-to-all-start.2 = ((bf16[4,8,55,128]{3,1,2,0:T(8,128)(2,1)}), bf16[4,8,55,128]{3,1,2,0:T(8,128)(2,1)S(1)}, u32[]{:S(2)}, u32[]{:S(2)}) async-start(bf16[4,8,55,128]{3,1,2,0:T(8,128)(2,1)} %copy.26), calls=%async_computation.2 | async-start | bytes 901120 | tf_op jit(solution)/shard_map/all_to_all | solution.py:89
  162.1 11.5 %all-to-all-start.3 = ((bf16[1,8,220,128]{3,1,0,2:T(8,128)(2,1)}), bf16[1,8,220,128]{3,1,0,2:T(8,128)(2,1)S(1)}, u32[]{:S(2)}, u32[]{:S(2)}) async-start(bf16[1,8,220,128]{3,1,0,2:T(8,128)(2,1)} %bitcast.90), calls=%async_computation.3 | async-start | bytes 901120 | tf_op jit(solution)/shard_map/all_to_all | solution.py:92
  165.6 156.8 %all-reduce.2.cloned.1.call-start = ((), (), s32[]{:S(2)}) async-start(), calls=%async_computation.7 | async-start | bytes 7340032 | tf_op jit(solution)/shard_map/psum | solution.py:59
  179.3 249.2 %all-gather.11.cloned.1.call-start = ((), (), s32[]{:S(2)}) async-start(), calls=%async_computation.9 | async-start | bytes 20971520 | tf_op jit(solution)/shard_map/all_gather | solution.py:28
  179.9 356.0 %all-gather.9.cloned.1.call-start = ((), (), s32[]{:S(2)}) async-start(), calls=%async_computation.8 | async-start | bytes 20971520 | tf_op jit(solution)/shard_map/all_gather | solution.py:22
  180.5 466.4 %reduce-scatter.2.cloned.1.call-start = ((), (), s32[]{:S(2)}) async-start(), calls=%async_computation.10 | async-start | bytes 4128768 | tf_op jit(solution)/shard_map/reduce_scatter | solution.py:70
  330.7 2.0 copy-start.1
Sparse Core Ops, SparseCore 0:
  12.7 84.7 all-gather.4
  99.1 39.4 all-gather.6
  179.4 142.8 all-reduce.1
  323.8 104.7 all-gather.10
  429.9 105.8 all-gather.8
  565.5 81.3 reduce-scatter.1
where the time goes:
time: 656 us
  waiting for transfers between devices  536 us (82%)
  matrix products  57.3 us (9%)
  other arithmetic  21.1 us (3%)
  starting transfers between devices  14.3 us (2%)
  between operations  13.6 us (2%)
  local copies, waits for them, and re-layouts  13 us (2%)
    all_gather x2, waiting for transfers between devices, project_rows(): lax.all_gather(weight, 'sp', axis=0, tiled=True)  182 us
    psum x1, waiting for transfers between devices, attention_combine(): lax.psum(partial_value.astype(jnp.bfloat16), 'tp').astype(jnp.float32)  142 us
    all_gather x2, waiting for transfers between devices, project_cols(): portion = lax.all_gather(weight, 'sp', axis=1, tiled=True)  94.7 us
    reduce_scatter x1, waiting for transfers between devices, mlp_combine(): lax.psum_scatter(partial_value.astype(jnp.bfloat16), 'tp', scatter_dimens...  81.5 us
    dot_general x2, matrix products, project_cols(): jnp.einsum(einsum_form, operand, shaped, preferred_element_type=jnp.float32)  35.2 us
    dot_general x1, matrix products, project_rows(): jnp.einsum(einsum_form, operand, lax.all_gather(weight, 'sp', axis=0, til...  18.3 us
    reduce_sum x2, other arithmetic, normalize(): center = jnp.mean(values, axis=-1, keepdims=True)  14.1 us
  transfers between devices with their start and end apart: 10, of which 9 were waited for; matrix products, arithmetic and copies ran while one was open for 7% of the time, Pallas kernels for 0%

commit v1 on v0

--- a/solution.py
+++ b/solution.py
@@ -5,6 +5,17 @@
 
 DH = 128
 EPSILON = 1e-06
+
+
+def turned_line(x, name, dim):
+    n_dev = lax.axis_size(name)
+    right = [(i, (i + 1) % n_dev) for i in range(n_dev)]
+    shards = [x]
+    for far in range(1, n_dev):
+        shards = [lax.ppermute(shards[0], name, right), *shards]
+    whole = jnp.concatenate(shards, axis=dim)
+    shift = (lax.axis_index(name) + 1) * shards[-1].shape[dim]
+    return jnp.roll(whole, shift, axis=dim)
 
 
 def normalize(tok_rows, shift_vec, scale_vec):
@@ -25,7 +36,7 @@
 
 
 def project_cols(operand, weight, einsum_form, leading):
-    portion = lax.all_gather(weight, "sp", axis=1, tiled=True)
+    portion = turned_line(weight, "sp", 1)
     shaped = portion.reshape(leading + (portion.shape[1],))
     return jnp.einsum(einsum_form, operand, shaped, preferred_element_type=jnp.float32)
 

time: 656 us -> 581 us (0.89); the launches traced: 656 us -> 573 us
  waiting for transfers between devices: 536 us -> 398 us
  local copies, waits for them, and re-layouts: 13 us -> 56.4 us
  starting transfers between devices: 14.3 us -> 23.2 us
    ppermute x0 -> x6, waiting for transfers between devices: none -> 181 us  [turned_line(): shards = [lax.ppermute(shards[0], name, right), *shards]]
    psum x1, waiting for transfers between devices: 142 us -> 0.01 us  [attention_combine(): lax.psum(partial_value.astype(jnp.bfloat16), 'tp').astype(jnp.float32)]
    all_gather x2 -> x0, waiting for transfers between devices: 94.7 us -> none  [project_cols(): portion = lax.all_gather(weight, 'sp', axis=1, tiled=True)]
    all_gather x2, waiting for transfers between devices: 182 us -> 125 us  [project_rows(): lax.all_gather(weight, 'sp', axis=0, tiled=True)]
    unnamed x7 -> x23, local copies, waits for them, and re-layouts: 5.18 us -> 33.4 us
    dot_general x2, matrix products: 35.2 us -> 18.5 us  [project_cols(): jnp.einsum(einsum_form, operand, shaped, preferred_element_type=jnp.float32)]
    dot_general x1 -> x2, matrix products: 18.3 us -> 31.9 us  [project_rows(): jnp.einsum(einsum_form, operand, lax.all_gather(weight, 'sp', axis=0, til...]
    all_to_all x1, waiting for transfers between devices: 12.3 us -> 2.67 us  [shards(): lax.all_to_all(projected[0], 'sp', split_axis=0, concat_axis=2, tiled=True)]
  transfers between devices with their start and end apart: 10 -> 14, of which waited for: 9 -> 12; matrix products, arithmetic and copies ran while one was open for 7% -> 15% of each run, Pallas kernels for 0% -> 0%
where the time goes in v1:
time: 581 us; the launch traced here: 573 us
  waiting for transfers between devices  398 us (69%)
  matrix products  59.2 us (10%)
  local copies, waits for them, and re-layouts  56.4 us (10%)
  starting transfers between devices  23.2 us (4%)
  other arithmetic  22.8 us (4%)
  between operations  13.6 us (2%)
    ppermute x6, waiting for transfers between devices, turned_line(): shards = [lax.ppermute(shards[0], name, right), *shards]  181 us
    all_gather x2, waiting for transfers between devices, project_rows(): lax.all_gather(weight, 'sp', axis=0, tiled=True)  125 us
    reduce_scatter x1, waiting for transfers between devices, mlp_combine(): lax.psum_scatter(partial_value.astype(jnp.bfloat16), 'tp', scatter_dimens...  81.5 us
    unnamed x23, local copies, waits for them, and re-layouts  33.4 us
    dot_general x2, matrix products, project_rows(): jnp.einsum(einsum_form, operand, lax.all_gather(weight, 'sp', axis=0, til...  31.9 us
    dot_general x2, matrix products, project_cols(): jnp.einsum(einsum_form, operand, shaped, preferred_element_type=jnp.float32)  18.5 us
    reduce_sum x2, other arithmetic, normalize(): center = jnp.mean(values, axis=-1, keepdims=True)  13.8 us
  transfers between devices with their start and end apart: 14, of which 12 were waited for; matrix products, arithmetic and copies ran while one was open for 15% of the time, Pallas kernels for 0%

profile of v1, /device:TPU:0, one launch (start us, length us, event | category | flops | bytes accessed | tf_op | source)
XLA Modules:
  0.0 573.4 jit_solution(4964862241632153725)
XLA Ops:
  6.5 3.2 copy.22
  9.7 2.8 copy.23
  13.1 5.6 convert_reduce_fusion
  18.8 5.9 %fusion.24 = f32[8,55]{1,0:T(8,128)S(1)} fusion(f32[8,55]{1,0:T(8,128)S(1)} %broadcast_multiply_fusion.1, bf16[8,55,4096]{2,0,1:T(8,128)(2,1)} %param.8), kind=kLoop, calls=%fused_computation.33 | loop fusion | flops 7208520 | bytes 3608000 | tf_op jit(solution)/shard_map/reduce_sum | solution.py:24
  24.7 3.1 collective-permute-done
  27.7 3.1 collective-permute-start.1
  30.9 33.6 %collective-permute-done.1 = bf16[512,1024]{1,0:T(8,128)(2,1)S(1)} collective-permute-done((bf16[512,1024]{1,0:T(8,128)(2,1)S(1)}, bf16[512,1024]{1,0:T(8,128)(2,1)S(1)}, u32[]{:S(2)}, u32[]{:S(2)}) %collective-permute-start.1) | collective-permute-done | bytes 1048608 | tf_op jit(solution)/shard_map/ppermute | solution.py:15
  64.6 3.4 collective-permute-start.2
  68.0 52.0 %all-gather.3.cloned.1.call-done = bf16[4096,3,4,128]{3,0,2,1:T(8,128)(2,1)} async-done(((bf16[1024,3,4,128]{3,0,2,1:T(8,128)(2,1)}), bf16[4096,3,4,128]{3,0,2,1:T(8,128)(2,1)}) %all-gather.3.cloned.1.call-update) | async-done | bytes 12582928 | tf_op jit(solution)/shard_map/all_gather | solution.py:33
  120.0 18.2 %fusion.65 = bf16[3,4,8,55,128]{4,3,1,0,2:T(8,128)(2,1)S(1)} fusion(bf16[4096,3,4,128]{3,0,2,1:T(8,128)(2,1)} %all-gather.3.cloned.1.call-done, f32[4096]{0:T(1024)S(1)} %bitcast.104, f32[4096]{0:T(1024)S(1)} %bitcast.105, f32[8,55]{1,0:T(8,128)S(1)} %add_rsqrt_fusion.1, f32[8,55]{1,0:T(8,128)S(1)} %broadcast_multiply_fusion.1, bf16[8,55,4096]{2,0,1:T(8,128)(2,1)} %param.8), kind=kOutput, calls=%fused_computation.64 | convolution fusion | flops 5547970560 | bytes 17575360 | tf_op jit(solution)/shard_map/fpd,dshe->shfpe/dot_general | solution.py:30
  138.3 1.1 slice_bitcast_fusion
  140.3 4.1 all-to-all-start.2
  144.5 2.3 constant_dynamic-update-slice_fusion.7
  147.8 2.0 copy.25
  149.8 2.7 all-to-all-done.2
  152.5 4.1 all-to-all-start.1
  158.8 2.3 constant_dynamic-update-slice_fusion.3
  161.1 2.0 copy.24
  163.1 1.7 all-to-all-done.1
  164.8 4.1 all-to-all-start
  168.9 1.1 constant_dynamic-update-slice_fusion.2
  173.2 1.1 copy.28
  174.3 2.7 all-to-all-done
  178.1 9.4 %while.10 = (s32[]{:T(128)}, bf16[8,220,128]{2,1,0:T(8,128)(2,1)}, bf16[8,220,128]{2,1,0:T(8,128)(2,1)S(1)}, bf16[8,220,128]{2,1,0:T(8,128)(2,1)S(1)}, bf16[8,220,128]{2,1,0:T(8,128)(2,1)S(1)}, /*index=5*/s32[]{:T(128)}) while((s32[]{:T(128)}, bf16[8,220,128]{2,1,0:T(8,128)(2,1)}, bf16[8,220,128]{2,1,0:T(8,128)(2,1)S(1)}, ...), condition=%wide.region_5.6_spmd, body=%wide.region_2.5_spmd.sunk | while | flops 25147320 | bytes 852765 | solution.py:65
  187.4 2.0 copy.52
  189.4 3.5 all-to-all-start.3
  192.9 4.7 constant_dynamic-slice_fusion.1
  197.6 3.3 all-to-all-done.3
  200.8 5.8 %bitcast_convert_fusion = bf16[8,55,4096]{2,1,0:T(8,128)(2,1)} fusion(bf16[4,128,4096,1]{2,1,0,3:T(8,128)(2,1)} %bitcast.99, bf16[1,8,4,55,128]{4,1,3,2,0:T(8,128)(2,1)S(1)} %bitcast.100), kind=kOutput, calls=%fused_computation.42 | convolution fusion | flops 1847296000 | bytes 8249344 | tf_op jit(solution)/shard_map/hfpd,hde->fpe/dot_general | solution.py:41
  207.5 48.1 %collective-permute-done.3 = bf16[2048,1024]{1,0:T(8,128)(2,1)S(1)} collective-permute-done((bf16[2048,1024]{1,0:T(8,128)(2,1)}, bf16[2048,1024]{1,0:T(8,128)(2,1)S(1)}, u32[]{:S(2)}, u32[]{:S(2)}) %collective-permute-start.3) | collective-permute-done | bytes 4194336 | tf_op jit(solution)/shard_map/ppermute | solution.py:15
  255.6 47.9 %collective-permute-done.4 = bf16[2048,1024]{1,0:T(8,128)(2,1)S(1)} collective-permute-done((bf16[2048,1024]{1,0:T(8,128)(2,1)S(1)}, bf16[2048,1024]{1,0:T(8,128)(2,1)S(1)}, u32[]{:S(2)}, u32[]{:S(2)}) %collective-permute-start.4) | collective-permute-done | bytes 4194336 | tf_op jit(solution)/shard_map/ppermute | solution.py:15
  303.7 47.9 %collective-permute-done.5 = bf16[2048,1024]{1,0:T(8,128)(2,1)S(1)} collective-permute-done((bf16[2048,1024]{1,0:T(8,128)(2,1)S(1)}, bf16[2048,1024]{1,0:T(8,128)(2,1)S(1)}, u32[]{:S(2)}, u32[]{:S(2)}) %collective-permute-start.5) | collective-permute-done | bytes 4194336 | tf_op jit(solution)/shard_map/ppermute | solution.py:15
  351.6 2.4 constant_dynamic-update-slice_fusion.15
  354.0 2.6 constant_dynamic-update-slice_fusion.14
  356.6 2.6 constant_dynamic-update-slice_fusion.13
  359.2 2.7 constant_dynamic-update-slice_fusion.12
  361.9 2.4 constant_dynamic-update-slice_fusion.11
  364.4 3.2 constant_dynamic-update-slice_fusion.10
  367.6 2.4 constant_dynamic-update-slice_fusion.9
  370.0 2.4 constant_dynamic-update-slice_fusion.8
  372.3 8.2 %convert_reduce_fusion.1 = (f32[8,55]{1,0:T(8,128)S(1)}, bf16[8,55,4096]{2,1,0:T(8,128)(2,1)S(1)}) fusion(bf16[8,55,4096]{2,1,0:T(8,128)(2,1)} %all-reduce.2.cloned.1.call-done, f32[4096]{0:T(1024)S(1)} %bitcast.101, bf16[8,55,4096]{2,0,1:T(8,128)(2,1)} %param.8), kind=kLoop, calls=%fused_computation.28 | loop fusion | flops 12615240 | bytes 10831584 | tf_op jit(solution)/shard_map/reduce_sum | solution.py:23
  380.6 1.8 copy-done.1
  382.4 1.1 fusion.28
  383.6 72.9 %all-gather.5.cloned.1.call-done = bf16[4096,2048]{1,0:T(8,128)(2,1)} async-done(((bf16[1024,2048]{1,0:T(8,128)(2,1)}), bf16[4096,2048]{1,0:T(8,128)(2,1)}) %all-gather.5.cloned.1.call-update) | async-done | bytes 16777232 | tf_op jit(solution)/shard_map/all_gather | solution.py:33
  456.5 13.7 %fusion.43 = bf16[8,55,2048]{2,1,0:T(8,128)(2,1)S(1)} fusion(bf16[4096,2048]{1,0:T(8,128)(2,1)} %all-gather.5.cloned.1.call-done, bf16[8,55,4096]{2,1,0:T(8,128)(2,1)} %copy-done.1, f32[4096]{0:T(1024)S(1)} %bitcast.102, f32[4096]{0:T(1024)S(1)} %bitcast.103, f32[8,55]{1,0:T(8,128)S(1)} %add_rsqrt_fusion, f32[8,55]{1,0:T(8,128)S(1)} %broadcast_multiply_fusion), kind=kOutput, calls=%fused_computation.52 | convolution fusion | flops 7400898560 | bytes 22220224 | tf_op jit(solution)/shard_map/fpd,dc->fpc/dot_general | solution.py:30
  470.2 12.7 %fusion.33 = bf16[8,55,4096]{2,1,0:T(8,128)(2,1)} fusion(bf16[8,55,2048]{2,1,0:T(8,128)(2,1)S(1)} %fusion.43, bf16[2048,8192]{1,0:T(8,128)(2,1)} %constant_dynamic-update-slice_fusion.8, s32[]{:T(128)S(6)} %select_n.24), kind=kOutput, calls=%fused_computation.43 | convolution fusion | flops 7383777280 | bytes 22183940 | tf_op jit(solution)/shard_map/fpk,kc->fpc/dot_general | solution.py:41
  482.9 81.5 %reduce-scatter.2.cloned.1.call-done = bf16[8,55,512]{2,1,0:T(8,128)(2,1)} async-done(((bf16[8,55,4096]{2,1,0:T(8,128)(2,1)}), bf16[8,55,512]{2,1,0:T(8,128)(2,1)}) %reduce-scatter.2.cloned.1.call-update) | async-done | bytes 450576 | tf_op jit(solution)/shard_map/reduce_scatter | solution.py:81
  564.4 1.3 add_convert_fusion
  (61 shorter events, 20.4 us)
Async XLA Ops:
  6.5 113.5 %all-gather.3.cloned.1.call-start = ((), (), s32[]{:S(2)}) async-start(), calls=%async_computation.5 | async-start | bytes 15728640 | tf_op jit(solution)/shard_map/all_gather | solution.py:33
  9.7 21.1 %copy-start.3 = (f32[6,4096]{1,0:T(8,128)S(1)}, f32[6,4096]{1,0:T(8,128)}, u32[]{:S(2)}) copy-start(f32[6,4096]{1,0:T(8,128)} %param.9) | copy-start | bytes 294916
  12.6 15.2 %collective-permute-start = (bf16[512,1024]{1,0:T(8,128)(2,1)}, bf16[512,1024]{1,0:T(8,128)(2,1)S(1)}, u32[]{:S(2)}, u32[]{:S(2)}) collective-permute-start(bf16[512,1024]{1,0:T(8,128)(2,1)} %param.11), channel_id=1, source_target_pairs={{0,8},{8,16},{16,24},{24,0},{1,9},{9,17},{17,25},{25,1},{2,10},{10... | collective-permute-start | bytes 3145736 | tf_op jit(solution)/shard_map/ppermute | solution.py:15
  27.7 36.8 %collective-permute-start.1 = (bf16[512,1024]{1,0:T(8,128)(2,1)S(1)}, bf16[512,1024]{1,0:T(8,128)(2,1)S(1)}, u32[]{:S(2)}, u32[]{:S(2)}) collective-permute-start(bf16[512,1024]{1,0:T(8,128)(2,1)S(1)} %collective-permute-done), channel_id=1, source_target_pairs={{0,8},{8,16},{16,24},{24,0},{1,9},{9,17},{17,25},{25,1},{2,10},{10... | collective-permute-start | bytes 3145736 | tf_op jit(solution)/shard_map/ppermute | solution.py:15
  64.6 79.9 %collective-permute-start.2 = (bf16[512,1024]{1,0:T(8,128)(2,1)S(1)}, bf16[512,1024]{1,0:T(8,128)(2,1)}, u32[]{:S(2)}, u32[]{:S(2)}) collective-permute-start(bf16[512,1024]{1,0:T(8,128)(2,1)S(1)} %collective-permute-done.1), channel_id=1, source_target_pairs={{0,8},{8,16},{16,24},{24,0},{1,9},{9,17},{17,25},{25,1},{2,10},{10... | collective-permute-start | bytes 3145736 | tf_op jit(solution)/shard_map/ppermute | solution.py:15
  138.3 19.5 %copy-start.2 = (bf16[512,1024]{1,0:T(8,128)(2,1)S(1)}, bf16[512,1024]{1,0:T(8,128)(2,1)}, u32[]{:S(2)}) copy-start(bf16[512,1024]{1,0:T(8,128)(2,1)} %param.11) | copy-start | bytes 3145732
  140.3 12.2 %all-to-all-start.2 = ((bf16[4,8,55,128]{3,1,2,0:T(8,128)(2,1)}), bf16[4,8,55,128]{3,1,2,0:T(8,128)(2,1)}, u32[]{:S(2)}, u32[]{:S(2)}) async-start(bf16[4,8,55,128]{3,1,2,0:T(8,128)(2,1)} %copy.26), calls=%async_computation.2 | async-start | bytes 901120 | tf_op jit(solution)/shard_map/all_to_all | solution.py:100
  152.5 12.2 %all-to-all-start.1 = ((bf16[4,8,55,128]{3,1,2,0:T(8,128)(2,1)}), bf16[4,8,55,128]{3,1,2,0:T(8,128)(2,1)}, u32[]{:S(2)}, u32[]{:S(2)}) async-start(bf16[4,8,55,128]{3,1,2,0:T(8,128)(2,1)} %copy.25), calls=%async_computation.1 | async-start | bytes 901120 | tf_op jit(solution)/shard_map/all_to_all | solution.py:99
  164.8 12.2 %all-to-all-start = ((bf16[4,8,55,128]{3,1,2,0:T(8,128)(2,1)}), bf16[4,8,55,128]{3,1,2,0:T(8,128)(2,1)}, u32[]{:S(2)}, u32[]{:S(2)}) async-start(bf16[4,8,55,128]{3,1,2,0:T(8,128)(2,1)} %copy.24), calls=%async_computation | async-start | bytes 901120 | tf_op jit(solution)/shard_map/all_to_all | solution.py:98
  189.4 11.5 %all-to-all-start.3 = ((bf16[1,8,220,128]{3,1,0,2:T(8,128)(2,1)}), bf16[1,8,220,128]{3,1,0,2:T(8,128)(2,1)S(1)}, u32[]{:S(2)}, u32[]{:S(2)}) async-start(bf16[1,8,220,128]{3,1,0,2:T(8,128)(2,1)} %bitcast.89), calls=%async_computation.3 | async-start | bytes 901120 | tf_op jit(solution)/shard_map/all_to_all | solution.py:103
  192.8 179.5 %all-reduce.2.cloned.1.call-start = ((), (), s32[]{:S(2)}) async-start(), calls=%async_computation.6 | async-start | bytes 7340032 | tf_op jit(solution)/shard_map/psum | solution.py:70
  206.6 249.9 %all-gather.5.cloned.1.call-start = ((), (), s32[]{:S(2)}) async-start(), calls=%async_computation.7 | async-start | bytes 20971520 | tf_op jit(solution)/shard_map/all_gather | solution.py:33
  207.4 357.1 %reduce-scatter.2.cloned.1.call-start = ((), (), s32[]{:S(2)}) async-start(), calls=%async_computation.8 | async-start | bytes 4128768 | tf_op jit(solution)/shard_map/reduce_scatter | solution.py:81
  207.4 48.2 %collective-permute-start.3 = (bf16[2048,1024]{1,0:T(8,128)(2,1)}, bf16[2048,1024]{1,0:T(8,128)(2,1)S(1)}, u32[]{:S(2)}, u32[]{:S(2)}) collective-permute-start(bf16[2048,1024]{1,0:T(8,128)(2,1)} %param.13), channel_id=1, source_target_pairs={{0,8},{8,16},{16,24},{24,0},{1,9},{9,17},{17,25},{25,1},{2,10},{10... | collective-permute-start | bytes 12582920 | tf_op jit(solution)/shard_map/ppermute | solution.py:15
  255.6 47.9 %collective-permute-start.4 = (bf16[2048,1024]{1,0:T(8,128)(2,1)S(1)}, bf16[2048,1024]{1,0:T(8,128)(2,1)S(1)}, u32[]{:S(2)}, u32[]{:S(2)}) collective-permute-start(bf16[2048,1024]{1,0:T(8,128)(2,1)S(1)} %collective-permute-done.3), channel_id=1, source_target_pairs={{0,8},{8,16},{16,24},{24,0},{1,9},{9,17},{17,25},{25,1},{2,10},{10... | collective-permute-start | bytes 12582920 | tf_op jit(solution)/shard_map/ppermute | solution.py:15
  303.5 48.1 %collective-permute-start.5 = (bf16[2048,1024]{1,0:T(8,128)(2,1)S(1)}, bf16[2048,1024]{1,0:T(8,128)(2,1)S(1)}, u32[]{:S(2)}, u32[]{:S(2)}) collective-permute-start(bf16[2048,1024]{1,0:T(8,128)(2,1)S(1)} %collective-permute-done.4), channel_id=1, source_target_pairs={{0,8},{8,16},{16,24},{24,0},{1,9},{9,17},{17,25},{25,1},{2,10},{10... | collective-permute-start | bytes 12582920 | tf_op jit(solution)/shard_map/ppermute | solution.py:15
  354.0 5.2 copy-start
  380.6 1.9 copy-start.1
Sparse Core Ops, SparseCore 0:
  12.7 107.2 all-gather.2
  206.7 143.3 all-reduce.1
  351.7 104.7 all-gather.4
  483.0 81.3 reduce-scatter.1
